TPU v7x, 32 devices: a whole 2x2x4 slice. The times are simulated.
32 devices in a mesh: row: 8 (over z, core), col: 4 (over y, x).
Axes of the slice: x: 2, y: 2, z: 4, core: 2. Of those that a mesh axis runs over, the one named last changes fastest.
Arguments:
- reflectivity: float32 [32, 256, 1024], P(('row', 'col')), may hold values from 0 to 40
- scan_hour: int32 [32], replicated, may hold values from 0 to 3, as said below
- basin_ids: int32 [256, 8], P('row', 'col'), may hold values from 0 to 255, as said below
Outputs:
- hourly_depth: float32 [4, 256, 1024], P(None, 'row', 'col')
- basin_depth: float32 [256, 4], P(('row', 'col'))
Inputs may be any that keep to these rules, and one draw needn't show every extreme that they name: scan_hour starts at 0, never falls, rises by at most one from one scan to the next, and every hour has 1 to 12 scans. `basin_ids`: every basin is named by at least one segment, and all segments of a basin lie in one aligned block of 8 grid rows.
All inputs are finite; a program needn't handle non-finite values.
Results may differ from a plain program's by a relative error of at most 0.00021.
Values sent between devices are 32-bit elements; how exact they have to be, the bound alone decides.
A program may use at most 64 MiB of HBM per device.

v0:
```python
import math

import jax
import jax.numpy as jnp
from jax import lax
from jax.sharding import PartitionSpec as P

SEG = 128
BASIN_ROWS = 8


slope_db = math.log(10.0) / 16.0
offset_zr = math.log(200.0) / 1.6


def rain_depth(reflect):
    return jnp.exp(reflect * slope_db - offset_zr) / 12.0


def body(reflectivity, scan_hour, basin_ids):
    row_devices = lax.axis_size("row")
    col_devices = lax.axis_size("col")
    scan_block, grid_height, grid_width = reflectivity.shape
    tile_rows = grid_height // row_devices
    tile_cols = grid_width // col_devices
    blocks = reflectivity.reshape(scan_block, row_devices, tile_rows, col_devices, tile_cols)
    blocks = blocks.transpose(0, 1, 3, 2, 4).reshape(
        scan_block, row_devices * col_devices, tile_rows, tile_cols
    )
    arrived = lax.all_to_all(blocks, ("row", "col"), split_axis=1, concat_axis=0, tiled=True)
    pixels = arrived.reshape(-1, tile_rows * tile_cols)
    pixels = rain_depth(pixels)
    hour_count = (scan_hour.shape[0] + 10) // 12 + 1
    selector = (scan_hour[None, :] == jnp.arange(hour_count, dtype=jnp.int32)[:, None]).astype(
        jnp.float32
    )
    hourly = jnp.dot(
        selector, pixels, precision=lax.Precision.HIGHEST, preferred_element_type=jnp.float32
    )
    segment = (
        hourly.reshape(hour_count, tile_rows, tile_cols // SEG, SEG)
        .sum(axis=3)
        .reshape(hour_count, -1)
    )
    basin_list = basin_ids.reshape(-1)
    basin_count = grid_height * grid_width // (SEG * BASIN_ROWS)
    members = (basin_list[:, None] == jnp.arange(basin_count, dtype=jnp.int32)[None, :]).astype(
        jnp.float32
    )
    partial_value = jnp.dot(
        members.T, segment.T, precision=lax.Precision.HIGHEST, preferred_element_type=jnp.float32
    )
    counts = jnp.sum(members, axis=0) * float(SEG)
    totals, basin_pixels = (
        lax.psum_scatter(partial_value, ("row", "col"), scatter_dimension=0, tiled=True),
        lax.psum_scatter(counts, ("row", "col"), scatter_dimension=0, tiled=True),
    )
    return (hourly.reshape(hour_count, tile_rows, tile_cols), totals / basin_pixels[:, None])


def solution(mesh):
    placed = (P(("row", "col"), None, None), P(), P("row", "col"))
    return jax.shard_map(
        body,
        mesh=mesh,
        in_specs=placed,
        out_specs=(P(None, "row", "col"), P(("row", "col"), None)),
        check_vma=False,
    )
```

profile of v0, /device:TPU:0, one launch (start us, length us, event | category | flops | bytes accessed | tf_op | source)
XLA Modules:
  0.0 81.1 jit_solution(17528979361150228671)
XLA Ops:
  0.6 1.7 %reshape.34 = f32[1,8,32,4,256]{4,3,2,1,0:T(4,128)S(1)} reshape(f32[1,256,1024]{2,1,0:T(8,128)} %param.3) | data formatting | bytes 2097152 | tf_op jit(solution)/shard_map/reshape | solution.py:26
  2.3 1.2 %copy.13 = f32[1,8,4,32,256]{4,3,2,1,0:T(8,128)} copy(f32[1,8,4,32,256]{4,2,3,1,0:T(4,128)S(1)} %bitcast.19) | data formatting | bytes 2097152 | tf_op jit(solution)/shard_map/transpose | solution.py:27
  3.5 7.3 %all-to-all-start = ((f32[1,32,32,256]{3,2,0,1:T(8,128)}), f32[1,32,32,256]{3,2,0,1:T(8,128)S(1)}, u32[]{:S(2)}, u32[]{:S(2)}) async-start(f32[1,32,32,256]{3,2,0,1:T(8,128)} %bitcast.2), calls=%async_computation | async-start | bytes 2097152 | tf_op jit(solution)/shard_map/all_to_all | solution.py:30
  10.8 0.0 copy-start
  10.9 0.7 copy-done
  11.5 0.1 copy.15
  11.6 0.1 eq.31
  11.7 0.1 convert_reduce_fusion
  11.8 25.5 %all-to-all-done = f32[1,32,32,256]{3,2,0,1:T(8,128)S(1)} async-done(((f32[1,32,32,256]{3,2,0,1:T(8,128)}), f32[1,32,32,256]{3,2,0,1:T(8,128)S(1)}, u32[]{:S(2)}, u32[]{:S(2)}) %all-to-all-start) | async-done | bytes 1048608 | tf_op jit(solution)/shard_map/all_to_all | solution.py:30
  37.4 0.2 exponential_multiply_fusion
  37.6 0.6 copy.19
  38.2 0.0 copy-start.1
  38.2 0.6 copy-done.1
  38.9 0.5 fusion.2
  39.3 0.1 reshape.37
  39.5 0.2 reduce_sum.18
  39.7 0.3 copy.16
  40.0 0.2 fusion
  40.2 0.7 copy.22
  40.9 39.4 %all-reduce.2 = (f32[256,4]{0,1:T(4,128)S(1)}, f32[256]{0:T(256)S(1)}) all-reduce(f32[256,4]{0,1:T(4,128)S(1)} %fusion, f32[256]{0:T(256)S(1)} %broadcast_multiply_fusion), channel_id=2, replica_groups=mesh['row'=8,'col'=4] {'row','col'}, use_global_device_ids=true, to_apply=%region_1.0.clone | all-reduce | flops 1280 | bytes 10240
  80.4 0.1 dynamic-slice.1
  80.4 0.7 dynamic-slice_divide_fusion
  (1 shorter events, 0.0 us)
Async XLA Ops:
  3.5 33.8 %all-to-all-start = ((f32[1,32,32,256]{3,2,0,1:T(8,128)}), f32[1,32,32,256]{3,2,0,1:T(8,128)S(1)}, u32[]{:S(2)}, u32[]{:S(2)}) async-start(f32[1,32,32,256]{3,2,0,1:T(8,128)} %bitcast.2), calls=%async_computation | async-start | bytes 2097152 | tf_op jit(solution)/shard_map/all_to_all | solution.py:30
  10.8 0.7 copy-start
  38.2 0.7 copy-start.1
where the time goes:
time: 81.4 us; the launch traced here: 81.1 us
  blocking collectives  39.4 us (48%)
  waiting for transfers between devices  25.5 us (31%)
  starting transfers between devices  7.33 us (9%)
  local copies, waits for them, and re-layouts  6.21 us (8%)
  other arithmetic  1.19 us (1%)
    unnamed x1, blocking collectives  39.4 us
    all_to_all x1, waiting for transfers between devices, body(): lax.all_to_all(blocks, ('row', 'col'), split_axis=1, concat_axis=0, tiled...  25.5 us
    all_to_all x1, starting transfers between devices, body(): lax.all_to_all(blocks, ('row', 'col'), split_axis=1, concat_axis=0, tiled...  7.33 us
    unnamed x8, local copies, waits for them, and re-layouts  2.78 us
    reshape x1, local copies, waits for them, and re-layouts, body(): reflectivity.reshape(scan_block, row_devices, tile_rows, col_devices, til...  1.7 us
  transfers between devices with their start and end apart: 1, of which 1 were waited for; matrix products, arithmetic and copies ran while one was open for 0% of the time, Pallas kernels for 0%

commit v1 on v0

v1 whole, which is shorter than its diff:
```python
import functools
import math

import jax
import jax.numpy as jnp
from jax import lax
from jax.experimental import pallas as pl
from jax.experimental.pallas import tpu as pltpu
from jax.sharding import PartitionSpec as P

SEG = 128
BASIN_ROWS = 8
HOUR_SCANS = 12
CORES = 2
MESH = pl.DeviceIdType.MESH

slope_db = math.log(10.0) / 16.0
offset_zr = math.log(200.0) / 1.6 + math.log(12.0)


def kernel(
    dims,
    refl_ref,
    hour_ref,
    ids_ref,
    hourly_ref,
    basin_ref,
    frame,
    hours,
    ids,
    gather,
    part,
    zrecv,
    psend,
    precv,
    local_sem,
    own_sem,
    in_send,
    in_recv,
    z_send,
    z_recv,
    b_send,
    b_recv,
):
    row_devices, col_devices, hour_count, slots, tile_rows, tile_cols, owned = dims
    planes = row_devices // CORES
    members = CORES * col_devices
    devices = row_devices * col_devices
    scan_block = gather.shape[2]
    scan_count = hour_ref.shape[0]
    plane_scans = members * scan_block
    segs = tile_cols // SEG

    row = lax.axis_index("row")
    col = lax.axis_index("col")
    plane = row // CORES
    core = row % CORES
    mine = core * col_devices + col
    me = row * col_devices + col

    def first_hour(p):
        return (p * plane_scans) // HOUR_SCANS

    def hour_span(p):
        tail = scan_count - plane_scans - p * plane_scans
        return hour_count - tail // HOUR_SCANS - first_hour(p)

    def member_at(k):
        other = (mine + k) % members
        return other, plane * CORES + other // col_devices, other % col_devices

    load_frame = pltpu.make_async_copy(refl_ref, frame, local_sem.at[0])
    load_hours = pltpu.make_async_copy(hour_ref, hours, local_sem.at[1])
    load_ids = pltpu.make_async_copy(ids_ref, ids, local_sem.at[2])
    load_frame.start()
    load_hours.start()
    load_ids.start()

    def block_of(source, d, c, q):
        rows = pl.ds(pl.multiple_of((d * CORES + c) * tile_rows, 8), tile_rows)
        cols = pl.ds(pl.multiple_of(q * tile_cols, 128), tile_cols)
        return source.at[:, rows, cols]

    barrier = pltpu.get_barrier_semaphore()
    for k in range(1, members):
        _, r, q = member_at(k)
        pl.semaphore_signal(barrier, inc=1, device_id=(r, q), device_id_type=MESH)
    for k in range(1, planes):
        r = ((plane + k) % planes) * CORES + core
        pl.semaphore_signal(barrier, inc=1, device_id=(r, col), device_id_type=MESH)

    own_copies = []
    for d in range(planes):
        own = pltpu.make_async_copy(
            block_of(refl_ref, d, core, col), gather.at[d, mine], own_sem.at[d]
        )
        own.start()
        own_copies.append(own)

    low = plane < planes // 2
    order = []
    for t in range(planes - 1):
        down = planes - 1 - t
        down = jnp.where(down > plane, down, down - 1)
        up = jnp.where(t < plane, t, t + 1)
        order.append(jnp.where(low, down, up))
    order.append(plane)

    pl.semaphore_wait(barrier, members - 1 + planes - 1)
    load_frame.wait()

    def in_copy(d, k):
        other, r, q = member_at(k)
        return pltpu.make_async_remote_copy(
            src_ref=block_of(frame, d, other // col_devices, q),
            dst_ref=gather.at[d, mine],
            send_sem=in_send.at[d, other],
            recv_sem=in_recv.at[d, mine],
            device_id=(r, q),
            device_id_type=MESH,
        )

    def in_arrival(d, k):
        other, r, q = member_at(k)
        return pltpu.make_async_remote_copy(
            src_ref=gather.at[d, other],
            dst_ref=gather.at[d, other],
            send_sem=in_send.at[d, other],
            recv_sem=in_recv.at[d, other],
            device_id=(r, q),
            device_id_type=MESH,
        )

    for d in order:
        for k in range(1, members):
            in_copy(d, k).start()

    load_hours.wait()
    load_ids.wait()
    for own in own_copies:
        own.wait()

    lane = lax.broadcasted_iota(jnp.int32, (tile_rows, 128), 1)
    owner_rows = lax.broadcasted_iota(jnp.int32, (devices, tile_rows), 0)
    owner_hot = []
    lane_hot = []
    for g in range(segs):
        id_row = ids[g : g + 1, :]
        owner = lax.div(id_row, jnp.full_like(id_row, owned))
        owner_hot.append((owner_rows == owner).astype(jnp.float32))
        within = (id_row - owner * owned).astype(jnp.float32)
        spread = jnp.transpose(jnp.broadcast_to(within, (128, tile_rows)))
        lane_hot.append(((lane % owned) == spread.astype(jnp.int32)).astype(jnp.float32))
    owner_all = jnp.concatenate(owner_hot, axis=1)

    base_hour = first_hour(plane)
    span = hour_span(plane)

    def z_copy(d, k):
        return pltpu.make_async_remote_copy(
            src_ref=part.at[d, k],
            dst_ref=zrecv.at[plane, k],
            send_sem=z_send.at[d, k],
            recv_sem=z_recv.at[plane, k],
            device_id=(d * CORES + core, col),
            device_id_type=MESH,
        )

    for t, d in enumerate(order):
        for k in range(1, members):
            in_arrival(d, k).wait_recv()
        sums = [jnp.zeros((tile_rows, tile_cols), jnp.float32)] * slots
        for i in range(members):
            for b in range(scan_block):
                hour = hours[plane * plane_scans + i * scan_block + b] - base_hour
                depth = jnp.exp(gather[d, i, b] * slope_db - offset_zr)
                for k in range(slots):
                    sums[k] = sums[k] + jnp.where(hour == k, depth, 0.0)
        if t < planes - 1:
            for k in range(slots):
                part[d, k] = sums[k]
            for k in range(slots):

                @pl.when(k < span)
                def _():
                    z_copy(d, k).start()
        else:
            for k in range(slots):
                zrecv[plane, k] = sums[k]

    for p in range(planes):

        @pl.when(p != plane)
        def _():
            for k in range(hour_span(p)):
                pltpu.make_async_remote_copy(
                    src_ref=zrecv.at[p, k],
                    dst_ref=zrecv.at[p, k],
                    send_sem=z_send.at[p, k],
                    recv_sem=z_recv.at[p, k],
                    device_id=(p * CORES + core, col),
                    device_id_type=MESH,
                ).wait_recv()

    lanes = [jnp.zeros((tile_rows, 128), jnp.float32) for _ in range(segs)]
    for h in range(hour_count):
        total = None
        for p in range(planes):
            if first_hour(p) <= h < first_hour(p) + hour_span(p):
                term = zrecv[p, h - first_hour(p)]
                total = term if total is None else total + term
        hourly_ref[h] = total
        for g in range(segs):
            value = jnp.sum(total[:, g * SEG : (g + 1) * SEG], axis=1, keepdims=True)
            lanes[g] = jnp.where(lane // owned == h, value, lanes[g])
    stacked = []
    for g in range(segs):
        filled = jnp.where(lane // owned == hour_count, float(SEG), lanes[g])
        stacked.append(filled * lane_hot[g])
    partial = lax.dot_general(
        owner_all,
        jnp.concatenate(stacked, axis=0),
        (((1,), (0,)), ((), ())),
        precision=lax.Precision.HIGHEST,
        preferred_element_type=jnp.float32,
    )
    for o in range(devices):
        psend[o] = partial[o : o + 1, :]

    def b_copy(k):
        other = (me + k) % devices
        return pltpu.make_async_remote_copy(
            src_ref=psend.at[other],
            dst_ref=precv.at[me],
            send_sem=b_send.at[other],
            recv_sem=b_recv.at[me],
            device_id=(other // col_devices, other % col_devices),
            device_id_type=MESH,
        )

    def b_start(k, carry):
        b_copy(k).start()
        return carry

    lax.fori_loop(1, devices, b_start, 0)
    precv[me] = psend[me]

    for d in order:
        for k in range(1, members):
            in_copy(d, k).wait_send()
    for d in order[:-1]:
        for k in range(slots):

            @pl.when(k < span)
            def _():
                z_copy(d, k).wait_send()

    def b_wait(k, carry):
        other = (me + k) % devices
        arrival = pltpu.make_async_remote_copy(
            src_ref=psend.at[other],
            dst_ref=precv.at[other],
            send_sem=b_send.at[other],
            recv_sem=b_recv.at[other],
            device_id=(other // col_devices, other % col_devices),
            device_id_type=MESH,
        )
        arrival.wait_recv()
        arrival.wait_send()
        return carry

    lax.fori_loop(1, devices, b_wait, 0)
    total = jnp.sum(precv[...], axis=0)
    count = total[:, hour_count * owned : (hour_count + 1) * owned]
    for h in range(hour_count):
        basin_ref[h : h + 1, :] = total[:, h * owned : (h + 1) * owned] / count


def body(reflectivity, scan_hour, basin_ids):
    row_devices = lax.axis_size("row")
    col_devices = lax.axis_size("col")
    scan_block, grid_height, grid_width = reflectivity.shape
    tile_rows = grid_height // row_devices
    tile_cols = grid_width // col_devices
    scan_count = scan_hour.shape[0]
    hour_count = (scan_count + 10) // HOUR_SCANS + 1
    devices = row_devices * col_devices
    owned = grid_height * grid_width // (SEG * BASIN_ROWS) // devices
    planes = row_devices // CORES
    members = CORES * col_devices
    plane_scans = members * scan_block
    slots = max(
        hour_count
        - (scan_count - plane_scans * (p + 1)) // HOUR_SCANS
        - (p * plane_scans) // HOUR_SCANS
        for p in range(planes)
    )
    dims = (row_devices, col_devices, hour_count, slots, tile_rows, tile_cols, owned)
    dma = pltpu.SemaphoreType.DMA
    f32 = jnp.float32
    anywhere = pl.BlockSpec(memory_space=pl.ANY)
    inside = pl.BlockSpec(memory_space=pltpu.VMEM)
    hourly, basin = pl.pallas_call(
        functools.partial(kernel, dims),
        out_shape=(
            jax.ShapeDtypeStruct((hour_count, tile_rows, tile_cols), f32),
            jax.ShapeDtypeStruct((hour_count, owned), f32),
        ),
        in_specs=[anywhere] * 3,
        out_specs=(inside, inside),
        scratch_shapes=[
            pltpu.VMEM(reflectivity.shape, f32),
            pltpu.SMEM(scan_hour.shape, jnp.int32),
            pltpu.VMEM(basin_ids.shape[::-1], jnp.int32),
            pltpu.VMEM((planes, members, scan_block, tile_rows, tile_cols), f32),
            pltpu.VMEM((planes, slots, tile_rows, tile_cols), f32),
            pltpu.VMEM((planes, slots, tile_rows, tile_cols), f32),
            pltpu.VMEM((devices, 1, 128), f32),
            pltpu.VMEM((devices, 1, 128), f32),
            dma((3,)),
            dma((planes,)),
            dma((planes, members)),
            dma((planes, members)),
            dma((planes, slots)),
            dma((planes, slots)),
            dma((devices,)),
            dma((devices,)),
        ],
        compiler_params=pltpu.CompilerParams(collective_id=0, has_side_effects=True),
    )(reflectivity, scan_hour, basin_ids.T)
    return hourly, basin.T


def solution(mesh):
    placed = (P(("row", "col"), None, None), P(), P("row", "col"))
    return jax.shard_map(
        body,
        mesh=mesh,
        in_specs=placed,
        out_specs=(P(None, "row", "col"), P(("row", "col"), None)),
        check_vma=False,
    )
```

time: 81.4 us -> 29.7 us (0.36)
  blocking collectives: 39.4 us -> 0 us
  Pallas kernels: 0 us -> 26.7 us
  waiting for transfers between devices: 25.5 us -> 0 us
  starting transfers between devices: 7.33 us -> 0 us
  local copies, waits for them, and re-layouts: 6.21 us -> 2.15 us
  other arithmetic: 1.19 us -> 0 us
    unnamed x1 -> x0, blocking collectives: 39.4 us -> none
    pallas_call x0 -> x1, Pallas kernels: none -> 26.7 us  [body(): pl.pallas_call(functools.partial(kernel, dims), out_shape=(jax.ShapeDtype...]
    all_to_all x1 -> x0, waiting for transfers between devices: 25.5 us -> none  [body(): lax.all_to_all(blocks, ('row', 'col'), split_axis=1, concat_axis=0, tiled...]
    all_to_all x1 -> x0, starting transfers between devices: 7.33 us -> none  [body(): lax.all_to_all(blocks, ('row', 'col'), split_axis=1, concat_axis=0, tiled...]
    reshape x2 -> x0, local copies, waits for them, and re-layouts: 1.84 us -> none  [the longest x1 1.7 us: body(): reflectivity.reshape(scan_block, row_devices, tile_rows, col_devices, til...]
    transpose x1 -> x0, local copies, waits for them, and re-layouts: 1.18 us -> none  [body(): blocks.transpose(0, 1, 3, 2, 4)]
    div x2 -> x0, other arithmetic: 0.89 us -> none  [the longest x1 0.65 us: body(): totals / basin_pixels[:, None]]
    unnamed x8 -> x4, local copies, waits for them, and re-layouts: 2.78 us -> 2.15 us
  transfers between devices with their start and end apart: 1 -> 0, of which waited for: 1 -> 0; matrix products, arithmetic and copies ran while one was open for 0% -> 0% of each run, Pallas kernels for 0% -> 0%
where the time goes in v1:
time: 29.7 us; the launch traced here: 29.5 us
  Pallas kernels  26.7 us (90%)
  local copies, waits for them, and re-layouts  2.15 us (7%)
  between operations  0.65 us (2%)
    pallas_call x1, Pallas kernels, body(): pl.pallas_call(functools.partial(kernel, dims), out_shape=(jax.ShapeDtype...  26.7 us
    unnamed x4, local copies, waits for them, and re-layouts  2.15 us

profile of v1, /device:TPU:0, one launch (start us, length us, event | category | flops | bytes accessed | tf_op | source)
XLA Modules:
  0.0 29.5 jit_solution(9502221993622026775)
XLA Ops:
  0.6 26.7 %shard_map.50 = (f32[4,32,256]{2,1,0:T(8,128)}, f32[4,8]{1,0:T(4,128)}) custom-call(f32[1,256,1024]{2,1,0:T(8,128)} %refl_ref.1, s32[32]{0:T(128)} %hour_ref.1, s32[2,32]{1,0:T(2,128)} %bitcast.3), custom_call_target="tpu_custom_call" | custom-call | tf_op jit(solution)/shard_map/pallas_call | solution.py:303
  27.4 0.0 copy-start
  27.4 1.6 %copy.7 = f32[4,32,256]{2,1,0:T(8,128)} copy(f32[4,32,256]{2,1,0:T(8,128)} %get-tuple-element.8) | data formatting | bytes 262144
  28.9 0.0 copy-done
  29.0 0.6 %copy.8 = f32[8,4]{0,1:T(4,128)} copy(f32[8,4]{0,1:T(4,128)S(1)} %bitcast.2) | data formatting | bytes 256
Async XLA Ops:
  27.4 1.6 %copy-start = (f32[4,8]{1,0:T(4,128)S(1)}, f32[4,8]{1,0:T(4,128)}, u32[]{:S(2)}) copy-start(f32[4,8]{1,0:T(4,128)} %get-tuple-element.5) | copy-start | bytes 388

commit v2 on v1

--- a/solution.py
+++ b/solution.py
@@ -31,14 +31,21 @@
     gather,
     part,
     zrecv,
+    plane_ids,
+    all_ids,
     psend,
     precv,
+    relay_sem,
     local_sem,
     own_sem,
     in_send,
     in_recv,
     z_send,
     z_recv,
+    id_send,
+    id_recv,
+    idz_send,
+    idz_recv,
     b_send,
     b_recv,
 ):
@@ -75,6 +82,10 @@
     load_frame.start()
     load_hours.start()
     load_ids.start()
+    load_own_ids = pltpu.make_async_copy(
+        ids_ref, plane_ids.at[core * col_devices + col], local_sem.at[3]
+    )
+    load_own_ids.start()
 
     def block_of(source, d, c, q):
         rows = pl.ds(pl.multiple_of((d * CORES + c) * tile_rows, 8), tile_rows)
@@ -85,9 +96,16 @@
     for k in range(1, members):
         _, r, q = member_at(k)
         pl.semaphore_signal(barrier, inc=1, device_id=(r, q), device_id_type=MESH)
-    for k in range(1, planes):
-        r = ((plane + k) % planes) * CORES + core
-        pl.semaphore_signal(barrier, inc=1, device_id=(r, col), device_id_type=MESH)
+    def along_z(step):
+        return ((plane + step) * CORES + core, col)
+
+    @pl.when(plane > 0)
+    def _():
+        pl.semaphore_signal(barrier, inc=1, device_id=along_z(-1), device_id_type=MESH)
+
+    @pl.when(plane < planes - 1)
+    def _():
+        pl.semaphore_signal(barrier, inc=1, device_id=along_z(1), device_id_type=MESH)
 
     own_copies = []
     for d in range(planes):
@@ -106,8 +124,24 @@
         order.append(jnp.where(low, down, up))
     order.append(plane)
 
-    pl.semaphore_wait(barrier, members - 1 + planes - 1)
+    load_ids.wait()
     load_frame.wait()
+    beside = jnp.where(plane > 0, 1, 0) + jnp.where(plane < planes - 1, 1, 0)
+    pl.semaphore_wait(barrier, members - 1 + beside)
+
+    def id_copy(k):
+        other, r, q = member_at(k)
+        return pltpu.make_async_remote_copy(
+            src_ref=ids,
+            dst_ref=plane_ids.at[mine],
+            send_sem=id_send.at[other],
+            recv_sem=id_recv.at[mine],
+            device_id=(r, q),
+            device_id_type=MESH,
+        )
+
+    for k in range(1, members):
+        id_copy(k).start()
 
     def in_copy(d, k):
         other, r, q = member_at(k)
@@ -131,27 +165,65 @@
             device_id_type=MESH,
         )
 
-    for d in order:
+    def send_chunk(d):
         for k in range(1, members):
             in_copy(d, k).start()
 
+    early = max(1, planes - 2)
+    for d in order[:early]:
+        send_chunk(d)
+
+    for j in range(planes - 2):
+
+        @pl.when(plane > 0)
+        def _():
+            pl.semaphore_signal(
+                relay_sem.at[1, j], inc=1, device_id=along_z(-1), device_id_type=MESH
+            )
+
+        @pl.when(plane < planes - 1)
+        def _():
+            pl.semaphore_signal(
+                relay_sem.at[0, j], inc=1, device_id=along_z(1), device_id_type=MESH
+            )
+
+        @pl.when(plane > 0)
+        def _():
+            pl.semaphore_wait(relay_sem.at[0, j], 1)
+
+        @pl.when(plane < planes - 1)
+        def _():
+            pl.semaphore_wait(relay_sem.at[1, j], 1)
+
+    for k in range(1, members):
+        other, r, q = member_at(k)
+        pltpu.make_async_remote_copy(
+            src_ref=ids,
+            dst_ref=plane_ids.at[other],
+            send_sem=id_send.at[other],
+            recv_sem=id_recv.at[other],
+            device_id=(r, q),
+            device_id_type=MESH,
+        ).wait_recv()
+    load_own_ids.wait()
+
+    def idz_copy(k, arrival=False):
+        other = (plane + k) % planes
+        return pltpu.make_async_remote_copy(
+            src_ref=plane_ids,
+            dst_ref=all_ids.at[other if arrival else plane],
+            send_sem=idz_send.at[other],
+            recv_sem=idz_recv.at[other if arrival else plane],
+            device_id=(other * CORES + core, col),
+            device_id_type=MESH,
+        )
+
+    for k in range(1, planes):
+        idz_copy(k).start()
+    all_ids[plane] = plane_ids[...]
     load_hours.wait()
-    load_ids.wait()
     for own in own_copies:
         own.wait()
-
-    lane = lax.broadcasted_iota(jnp.int32, (tile_rows, 128), 1)
-    owner_rows = lax.broadcasted_iota(jnp.int32, (devices, tile_rows), 0)
-    owner_hot = []
-    lane_hot = []
-    for g in range(segs):
-        id_row = ids[g : g + 1, :]
-        owner = lax.div(id_row, jnp.full_like(id_row, owned))
-        owner_hot.append((owner_rows == owner).astype(jnp.float32))
-        within = (id_row - owner * owned).astype(jnp.float32)
-        spread = jnp.transpose(jnp.broadcast_to(within, (128, tile_rows)))
-        lane_hot.append(((lane % owned) == spread.astype(jnp.int32)).astype(jnp.float32))
-    owner_all = jnp.concatenate(owner_hot, axis=1)
 
     base_hour = first_hour(plane)
     span = hour_span(plane)
@@ -166,7 +238,63 @@
             device_id_type=MESH,
         )
 
+    def b_copy(k):
+        other = (me + k) % devices
+        return pltpu.make_async_remote_copy(
+            src_ref=psend,
+            dst_ref=precv.at[me],
+            send_sem=b_send.at[other],
+            recv_sem=b_recv.at[me],
+            device_id=(other // col_devices, other % col_devices),
+            device_id_type=MESH,
+        )
+
+    basins = psend.shape[1]
+
+    def sum_basins():
+        lane = lax.broadcasted_iota(jnp.int32, (tile_rows, basins), 1)
+
+        def row_block(r, carry):
+            count, *totals = carry
+            p = r // CORES
+            c = r % CORES
+            depths = []
+            for b in range(scan_block):
+                rows = pl.ds(pl.multiple_of(r * tile_rows, 8), tile_rows)
+                depths.append(jnp.exp(frame[b, rows, :] * slope_db - offset_zr))
+            tiles = [all_ids[p, c * col_devices + q] for q in range(col_devices)]
+            columns = jnp.transpose(jnp.concatenate(tiles, axis=0).astype(jnp.float32))
+            columns = columns.astype(jnp.int32)
+            for g in range(segs * col_devices):
+                hit = columns[:, g : g + 1] == lane
+                count = count + jnp.where(hit, float(SEG), 0.0)
+                for b in range(scan_block):
+                    part_depth = depths[b][:, g * SEG : (g + 1) * SEG]
+                    value = jnp.sum(part_depth, axis=1, keepdims=True)
+                    totals[b] = totals[b] + jnp.where(hit, value, 0.0)
+            return (count, *totals)
+
+        zero = jnp.zeros((tile_rows, basins), jnp.float32)
+        count, *totals = lax.fori_loop(0, row_devices, row_block, (zero,) * (scan_block + 1))
+        for b in range(scan_block):
+            psend[b : b + 1, :] = jnp.sum(totals[b], axis=0, keepdims=True)
+        return jnp.sum(count, axis=0, keepdims=True)
+
+    count = None
     for t, d in enumerate(order):
+        if t == min(1, planes - 1):
+            for k in range(1, planes):
+                idz_copy(k, arrival=True).wait_recv()
+            count = sum_basins()
+
+            def b_start(k, carry):
+                b_copy(k).start()
+                return carry
+
+            lax.fori_loop(1, devices, b_start, 0)
+            precv[me] = psend[...]
+            for late in order[early + 1 :]:
+                send_chunk(late)
         for k in range(1, members):
             in_arrival(d, k).wait_recv()
         sums = [jnp.zeros((tile_rows, tile_cols), jnp.float32)] * slots
@@ -184,6 +312,9 @@
                 @pl.when(k < span)
                 def _():
                     z_copy(d, k).start()
+
+            if t == 0:
+                send_chunk(order[early])
         else:
             for k in range(slots):
                 zrecv[plane, k] = sums[k]
@@ -202,7 +333,6 @@
                     device_id_type=MESH,
                 ).wait_recv()
 
-    lanes = [jnp.zeros((tile_rows, 128), jnp.float32) for _ in range(segs)]
     for h in range(hour_count):
         total = None
         for p in range(planes):
@@ -210,41 +340,11 @@
                 term = zrecv[p, h - first_hour(p)]
                 total = term if total is None else total + term
         hourly_ref[h] = total
-        for g in range(segs):
-            value = jnp.sum(total[:, g * SEG : (g + 1) * SEG], axis=1, keepdims=True)
-            lanes[g] = jnp.where(lane // owned == h, value, lanes[g])
-    stacked = []
-    for g in range(segs):
-        filled = jnp.where(lane // owned == hour_count, float(SEG), lanes[g])
-        stacked.append(filled * lane_hot[g])
-    partial = lax.dot_general(
-        owner_all,
-        jnp.concatenate(stacked, axis=0),
-        (((1,), (0,)), ((), ())),
-        precision=lax.Precision.HIGHEST,
-        preferred_element_type=jnp.float32,
-    )
-    for o in range(devices):
-        psend[o] = partial[o : o + 1, :]
-
-    def b_copy(k):
-        other = (me + k) % devices
-        return pltpu.make_async_remote_copy(
-            src_ref=psend.at[other],
-            dst_ref=precv.at[me],
-            send_sem=b_send.at[other],
-            recv_sem=b_recv.at[me],
-            device_id=(other // col_devices, other % col_devices),
-            device_id_type=MESH,
-        )
-
-    def b_start(k, carry):
-        b_copy(k).start()
-        return carry
-
-    lax.fori_loop(1, devices, b_start, 0)
-    precv[me] = psend[me]
-
+
+    for k in range(1, members):
+        id_copy(k).wait_send()
+    for k in range(1, planes):
+        idz_copy(k).wait_send()
     for d in order:
         for k in range(1, members):
             in_copy(d, k).wait_send()
@@ -258,7 +358,7 @@
     def b_wait(k, carry):
         other = (me + k) % devices
         arrival = pltpu.make_async_remote_copy(
-            src_ref=psend.at[other],
+            src_ref=psend,
             dst_ref=precv.at[other],
             send_sem=b_send.at[other],
             recv_sem=b_recv.at[other],
@@ -270,10 +370,15 @@
         return carry
 
     lax.fori_loop(1, devices, b_wait, 0)
-    total = jnp.sum(precv[...], axis=0)
-    count = total[:, hour_count * owned : (hour_count + 1) * owned]
-    for h in range(hour_count):
-        basin_ref[h : h + 1, :] = total[:, h * owned : (h + 1) * owned] / count
+    hour_rows = lax.broadcasted_iota(jnp.int32, (hour_count, basins), 0)
+    total = jnp.zeros((hour_count, basins), jnp.float32)
+    for o in range(devices):
+        for b in range(scan_block):
+            hour = hours[o * scan_block + b]
+            total = total + jnp.where(hour_rows == hour, precv[o, b : b + 1, :], 0.0)
+    mean = total / count
+    mean = pltpu.roll(mean, (basins - me * owned) % basins, 1)
+    basin_ref[...] = mean[:, :owned]
 
 
 def body(reflectivity, scan_hour, basin_ids):
@@ -298,7 +403,7 @@
     dims = (row_devices, col_devices, hour_count, slots, tile_rows, tile_cols, owned)
     dma = pltpu.SemaphoreType.DMA
     f32 = jnp.float32
-    anywhere = pl.BlockSpec(memory_space=pl.ANY)
+    anywhere = pl.BlockSpec(memory_space=pltpu.HBM)
     inside = pl.BlockSpec(memory_space=pltpu.VMEM)
     hourly, basin = pl.pallas_call(
         functools.partial(kernel, dims),
@@ -315,18 +420,27 @@
             pltpu.VMEM((planes, members, scan_block, tile_rows, tile_cols), f32),
             pltpu.VMEM((planes, slots, tile_rows, tile_cols), f32),
             pltpu.VMEM((planes, slots, tile_rows, tile_cols), f32),
-            pltpu.VMEM((devices, 1, 128), f32),
-            pltpu.VMEM((devices, 1, 128), f32),
-            dma((3,)),
+            pltpu.VMEM((members,) + basin_ids.shape[::-1], jnp.int32),
+            pltpu.VMEM((planes, members) + basin_ids.shape[::-1], jnp.int32),
+            pltpu.VMEM((scan_block, devices * owned), f32),
+            pltpu.VMEM((devices, scan_block, devices * owned), f32),
+            pltpu.SemaphoreType.REGULAR((2, max(1, planes - 2))),
+            dma((4,)),
             dma((planes,)),
             dma((planes, members)),
             dma((planes, members)),
             dma((planes, slots)),
             dma((planes, slots)),
+            dma((members,)),
+            dma((members,)),
+            dma((planes,)),
+            dma((planes,)),
             dma((devices,)),
             dma((devices,)),
         ],
-        compiler_params=pltpu.CompilerParams(collective_id=0, has_side_effects=True),
+        compiler_params=pltpu.CompilerParams(
+            collective_id=0, has_side_effects=True, vmem_limit_bytes=40 * 2**20
+        ),
     )(reflectivity, scan_hour, basin_ids.T)
     return hourly, basin.T
 

time: 29.7 us -> 26.9 us (0.906)
  Pallas kernels: 26.7 us -> 22.9 us
  local copies, waits for them, and re-layouts: 2.15 us -> 3.13 us
    pallas_call x1, Pallas kernels: 26.7 us -> 22.9 us  [body(): pl.pallas_call(functools.partial(kernel, dims), out_shape=(jax.ShapeDtype...]
    unnamed x4 -> x8, local copies, waits for them, and re-layouts: 2.15 us -> 3.13 us
where the time goes in v2:
time: 26.9 us; the launch traced here: 26.7 us
  Pallas kernels  22.9 us (85%)
  local copies, waits for them, and re-layouts  3.13 us (12%)
  between operations  0.66 us (2%)
    pallas_call x1, Pallas kernels, body(): pl.pallas_call(functools.partial(kernel, dims), out_shape=(jax.ShapeDtype...  22.9 us
    unnamed x8, local copies, waits for them, and re-layouts  3.13 us

profile of v2, /device:TPU:0, one launch (start us, length us, event | category | flops | bytes accessed | tf_op | source)
XLA Modules:
  0.0 26.7 jit_solution(5112479875266010212)
XLA Ops:
  0.6 0.0 copy-start.1
  0.6 0.0 copy-start.2
  0.6 0.7 %copy-done.1 = s32[32,2]{0,1:T(2,128)S(1)} copy-done((s32[32,2]{0,1:T(2,128)S(1)}, s32[32,2]{0,1:T(2,128)}, u32[]{:S(2)}) %copy-start.1) | copy-done | bytes 280
  1.3 0.0 copy-done.2
  1.3 0.0 copy-start
  1.3 1.2 %copy-done = f32[1,256,1024]{2,1,0:T(8,128)S(1)} copy-done((f32[1,256,1024]{2,1,0:T(8,128)S(1)}, f32[1,256,1024]{2,1,0:T(8,128)}, u32[]{:S(2)}) %copy-start) | copy-done | bytes 1048600
  2.5 22.9 %shard_map.50 = (f32[4,32,256]{2,1,0:T(8,128)S(1)}, f32[4,8]{1,0:T(4,128)S(1)}) custom-call(f32[1,256,1024]{2,1,0:T(8,128)S(1)} %copy-done, s32[32]{0:T(128)S(1)} %copy-done.2, s32[2,32]{1,0:T(2,128)S(1)} %bitcast.3), custom_call_target="tpu_custom_call" | custom-call | tf_op jit(solution)/shard_map/pallas_call | solution.py:408
  25.5 0.7 %copy.7 = f32[4,32,256]{2,1,0:T(8,128)} copy(f32[4,32,256]{2,1,0:T(8,128)S(1)} %get-tuple-element.8) | data formatting | bytes 262144
  26.2 0.6 %copy.8 = f32[8,4]{0,1:T(4,128)} copy(f32[8,4]{0,1:T(4,128)S(1)} %bitcast.2) | data formatting | bytes 256
Async XLA Ops:
  0.6 0.7 %copy-start.1 = (s32[32,2]{0,1:T(2,128)S(1)}, s32[32,2]{0,1:T(2,128)}, u32[]{:S(2)}) copy-start(s32[32,2]{0,1:T(2,128)} %param.5) | copy-start | bytes 772
  0.6 0.7 %copy-start.2 = (s32[32]{0:T(128)S(1)}, s32[32]{0:T(128)}, u32[]{:S(2)}) copy-start(s32[32]{0:T(128)} %hour_ref.1) | copy-start | bytes 388
  1.3 1.2 %copy-start = (f32[1,256,1024]{2,1,0:T(8,128)S(1)}, f32[1,256,1024]{2,1,0:T(8,128)}, u32[]{:S(2)}) copy-start(f32[1,256,1024]{2,1,0:T(8,128)} %refl_ref.1) | copy-start | bytes 3145732

commit v3 on v2

--- a/solution.py
+++ b/solution.py
@@ -73,7 +73,11 @@
         return hour_count - tail // HOUR_SCANS - first_hour(p)
 
     def member_at(k):
-        other = (mine + k) % members
+        dc = k // col_devices
+        dq = k % col_devices
+        half = col_devices // 2
+        qq = ((col // 2 + dq // 2) % half) * 2 + (col + dq) % 2
+        other = ((core + dc) % CORES) * col_devices + qq
         return other, plane * CORES + other // col_devices, other % col_devices
 
     load_frame = pltpu.make_async_copy(refl_ref, frame, local_sem.at[0])
@@ -169,7 +173,7 @@
         for k in range(1, members):
             in_copy(d, k).start()
 
-    early = max(1, planes - 2)
+    early = max(1, planes - 1)
     for d in order[:early]:
         send_chunk(d)
 
@@ -275,7 +279,9 @@
             return (count, *totals)
 
         zero = jnp.zeros((tile_rows, basins), jnp.float32)
-        count, *totals = lax.fori_loop(0, row_devices, row_block, (zero,) * (scan_block + 1))
+        count, *totals = lax.fori_loop(
+            0, row_devices, row_block, (zero,) * (scan_block + 1), unroll=4
+        )
         for b in range(scan_block):
             psend[b : b + 1, :] = jnp.sum(totals[b], axis=0, keepdims=True)
         return jnp.sum(count, axis=0, keepdims=True)
@@ -291,9 +297,9 @@
                 b_copy(k).start()
                 return carry
 
-            lax.fori_loop(1, devices, b_start, 0)
+            lax.fori_loop(1, devices, b_start, 0, unroll=True)
             precv[me] = psend[...]
-            for late in order[early + 1 :]:
+            for late in order[early:]:
                 send_chunk(late)
         for k in range(1, members):
             in_arrival(d, k).wait_recv()
@@ -313,8 +319,6 @@
                 def _():
                     z_copy(d, k).start()
 
-            if t == 0:
-                send_chunk(order[early])
         else:
             for k in range(slots):
                 zrecv[plane, k] = sums[k]
@@ -369,7 +373,7 @@
         arrival.wait_send()
         return carry
 
-    lax.fori_loop(1, devices, b_wait, 0)
+    lax.fori_loop(1, devices, b_wait, 0, unroll=True)
     hour_rows = lax.broadcasted_iota(jnp.int32, (hour_count, basins), 0)
     total = jnp.zeros((hour_count, basins), jnp.float32)
     for o in range(devices):
@@ -379,6 +383,15 @@
     mean = total / count
     mean = pltpu.roll(mean, (basins - me * owned) % basins, 1)
     basin_ref[...] = mean[:, :owned]
+
+
+def write_out(hourly_ref, basin_ref, hourly_out, basin_out, sem):
+    pairs = ((hourly_ref, hourly_out), (basin_ref, basin_out))
+    copies = [pltpu.make_async_copy(s, d, sem.at[n]) for n, (s, d) in enumerate(pairs)]
+    for copy in copies:
+        copy.start()
+    for copy in copies:
+        copy.wait()
 
 
 def body(reflectivity, scan_hour, basin_ids):
@@ -441,7 +454,18 @@
         compiler_params=pltpu.CompilerParams(
             collective_id=0, has_side_effects=True, vmem_limit_bytes=40 * 2**20
         ),
-    )(reflectivity, scan_hour, basin_ids.T)
+    )(*(pltpu.with_memory_space_constraint(v, pltpu.HBM) for v in (reflectivity, scan_hour, basin_ids.T)))
+    hourly, basin = pl.pallas_call(
+        write_out,
+        out_shape=(
+            jax.ShapeDtypeStruct(hourly.shape, f32),
+            jax.ShapeDtypeStruct(basin.shape, f32),
+        ),
+        in_specs=[inside] * 2,
+        out_specs=(anywhere, anywhere),
+        scratch_shapes=[dma((2,))],
+        compiler_params=pltpu.CompilerParams(vmem_limit_bytes=8 * 2**20),
+    )(hourly, basin)
     return hourly, basin.T
 
 

time: 26.9 us -> 23 us (0.86)
  local copies, waits for them, and re-layouts: 3.13 us -> 0 us
  Pallas kernels: 22.9 us -> 22.2 us
    unnamed x8 -> x0, local copies, waits for them, and re-layouts: 3.13 us -> none
    pallas_call x1, Pallas kernels: 22.9 us -> 21.5 us  [body(): pl.pallas_call(functools.partial(kernel, dims), out_shape=(jax.ShapeDtype...]
    pallas_call x0 -> x1, Pallas kernels: none -> 0.68 us  [body(): pl.pallas_call(write_out, out_shape=(jax.ShapeDtypeStruct(hourly.shape, f...]
where the time goes in v3:
time: 23 us; the launch traced here: 22.8 us
  Pallas kernels  22.2 us (97%)
  between operations  0.64 us (3%)
    pallas_call x1, Pallas kernels, body(): pl.pallas_call(functools.partial(kernel, dims), out_shape=(jax.ShapeDtype...  21.5 us
    pallas_call x1, Pallas kernels, body(): pl.pallas_call(write_out, out_shape=(jax.ShapeDtypeStruct(hourly.shape, f...  0.68 us

profile of v3, /device:TPU:0, one launch (start us, length us, event | category | flops | bytes accessed | tf_op | source)
XLA Modules:
  0.0 22.8 jit_solution(7670245870127882282)
XLA Ops:
  0.6 21.5 %shard_map.50 = (f32[4,32,256]{2,1,0:T(8,128)S(1)}, f32[4,8]{1,0:T(4,128)S(1)}) custom-call(f32[1,256,1024]{2,1,0:T(8,128)} %refl_ref.1, s32[32]{0:T(128)} %hour_ref.1, s32[2,32]{1,0:T(2,128)} %bitcast.2), custom_call_target="tpu_custom_call" | custom-call | tf_op jit(solution)/shard_map/pallas_call | solution.py:421
  22.1 0.7 %shard_map.51 = (f32[4,32,256]{2,1,0:T(8,128)}, f32[4,8]{1,0:T(4,128)}) custom-call(f32[4,32,256]{2,1,0:T(8,128)S(1)} %get-tuple-element.6.hourly_ref, f32[4,8]{1,0:T(4,128)S(1)} %get-tuple-element.7.basin_ref), custom_call_target="tpu_custom_call" | custom-call | tf_op jit(solution)/shard_map/pallas_call | solution.py:458
